TPU v7x, 512 devices: a whole 4x8x8 slice. The times are simulated.
512 devices in a mesh: dp: 16 (over x, y_lo, core), pipe: 8 (over z), tensor: 4 (over y_hi).
Axes of the slice: x: 4, y: 8 (y_hi: 4, y_lo: 2; y = y_hi * 2 + y_lo), z: 8, core: 2. Of those that a mesh axis runs over, the one named last changes fastest.
Arguments:
- weights: bfloat16 [11264, 1408], P(('dp', 'pipe', 'tensor')), may hold values from -6 to 6
- first_moment: bfloat16 [11264, 1408], P(('dp', 'pipe', 'tensor')), may hold values from -6 to 6
- second_moment: bfloat16 [11264, 1408], P(('dp', 'pipe', 'tensor')), may hold values from 0.049804688 to 5
- row_weight: float32 [1408], replicated, may hold values from -1 to 1
- col_weight: float32 [1408], replicated, may hold values from 1 to 4
Outputs:
- weight_tiles: bfloat16 [11264, 1408], P(('pipe', 'tensor'))
- first_tiles: bfloat16 [11264, 1408], P(('pipe', 'tensor'))
- second_tiles: bfloat16 [11264, 1408], P(('pipe', 'tensor'))
- checksums: float32 [3, 8, 4, 11], P(None, 'pipe', 'tensor')
All inputs are finite; a program needn't handle non-finite values.
Results may differ from a plain program's by a relative error of at most 0.001.
Values may be sent and summed in bfloat16 or wider, within the bound.
A program may use at most 64 MiB of HBM per device.

v0:
```python
import jax
import jax.numpy as jnp
from jax import lax
from jax.sharding import Mesh
from jax.sharding import PartitionSpec as P

CHECK_COLS = 128
DP = ("dp_0", "dp_1", "dp_2")
DP_PIPE_TENSOR = ("dp_0", "dp_1", "dp_2", "pipe", "tensor")


def for_sending(array):
    return jax.tree.map(lambda a: a.astype(jnp.bfloat16) if a.dtype == jnp.float32 else a, array)


def laid_out(blocks, dim):
    dims = list(blocks.shape[1:])
    dims[dim] *= blocks.shape[0]
    return jnp.moveaxis(blocks, 0, dim).reshape(dims)


def gather_in_order(array, axes, order):
    blocks = array[None]
    for k in order:
        blocks = lax.all_gather(blocks, axes[k], axis=0, tiled=True)
    block = [lax.axis_size(axes[k]) for k in reversed(order)]
    blocks = blocks.reshape(*block, *array.shape)
    turned = sorted(range(len(order)), key=lambda place: order[len(order) - 1 - place])
    return blocks.transpose(*turned, *range(len(order), blocks.ndim)).reshape(-1, *array.shape)


def gather_axes(array, axes, order, dim):
    return laid_out(gather_in_order(array, axes, order), dim)


def column_sums(data, row_part, col_weight, col_blocks):
    row_mixed = jnp.dot(
        row_part[None, :], data.astype(jnp.float32), precision=lax.Precision.HIGHEST
    )[0]
    return jnp.sum((row_mixed * col_weight).reshape(col_blocks, -1), axis=1)


def shards(weights, first_moment, second_moment, row_weight, col_weight):
    dp_count = lax.axis_size(DP)
    pipe_count = lax.axis_size("pipe")
    tensor_count = lax.axis_size("tensor")
    shard_rows, width = weights.shape
    dp_section = dp_count // pipe_count
    tile_shards = dp_count // tensor_count
    piece_cols = width // dp_count
    tile_rows = shard_rows * dp_count
    col_blocks = width // CHECK_COLS
    factor = float(tile_rows * CHECK_COLS) ** (-0.5)
    sources = (weights, first_moment, second_moment)
    exchanged = (
        lax.all_to_all(sources[0], DP, split_axis=1, concat_axis=0, tiled=True),
        lax.all_to_all(sources[1], DP, split_axis=1, concat_axis=0, tiled=True),
        lax.all_to_all(sources[2], DP, split_axis=1, concat_axis=0, tiled=True),
    )
    grouped = tuple(
        (item.reshape(pipe_count, dp_section, shard_rows, piece_cols) for item in exchanged)
    )
    sectioned = jax.tree.map(
        lambda part, own: part.astype(own.dtype),
        lax.all_to_all(for_sending(grouped), "pipe", split_axis=0, concat_axis=2, tiled=True),
        grouped,
    )
    routed = tuple(
        (item.reshape(tensor_count, tile_shards, 1, shard_rows, piece_cols) for item in sectioned)
    )
    arrived = jax.tree.map(
        lambda part, own: part.astype(own.dtype),
        lax.all_to_all(for_sending(routed), "tensor", split_axis=0, concat_axis=2, tiled=True),
        routed,
    )
    flat_pieces = tuple((item.reshape(tile_rows, piece_cols) for item in arrived))
    tiles = jax.tree.map(
        lambda part, own: part.astype(own.dtype),
        jax.tree.map(lambda part: gather_axes(part, DP, (1, 0, 2), 1), for_sending(flat_pieces)),
        flat_pieces,
    )
    tensor_pos = lax.axis_index("tensor")
    row_part = lax.dynamic_slice_in_dim(row_weight, tensor_pos * tile_rows, tile_rows)
    local_sums = jnp.stack([column_sums(item, row_part, col_weight, col_blocks) for item in tiles])
    checks = (local_sums * factor).reshape(3, 1, 1, col_blocks)
    return (tiles[0], tiles[1], tiles[2], checks)


def solution(mesh):
    finer = Mesh(
        mesh.devices.reshape(4, 2, 2, mesh.shape["pipe"], mesh.shape["tensor"]),
        ("dp_0", "dp_1", "dp_2", "pipe", "tensor"),
    )
    in_specs = (P(DP_PIPE_TENSOR, None), P(DP_PIPE_TENSOR, None), P(DP_PIPE_TENSOR, None), P(), P())
    out_specs = (
        P(("pipe", "tensor"), None),
        P(("pipe", "tensor"), None),
        P(("pipe", "tensor"), None),
        P(None, "pipe", "tensor", None),
    )
    return jax.shard_map(
        shards, mesh=finer, in_specs=in_specs, out_specs=out_specs, check_vma=False
    )
```

profile of v0, /device:TPU:1, one launch (start us, length us, event | category | flops | bytes accessed | tf_op | source)
XLA Modules:
  0.0 177.1 jit_solution(7908738768736243178)
XLA Ops:
  0.6 1.1 all_to_all.102
  2.4 10.1 %all-to-all-start = ((bf16[22,16,88]{2,0,1:T(8,128)(2,1)}), bf16[22,16,88]{2,0,1:T(8,128)(2,1)S(1)}, u32[]{:S(2)}, u32[]{:S(2)}) async-start(bf16[22,16,88]{2,0,1:T(8,128)(2,1)} %copy.84), calls=%async_computation | async-start | bytes 196608 | tf_op jit(solution)/shard_map/all_to_all | solution.py:56
  12.5 1.1 all_to_all.111
  14.3 4.2 %all-to-all-done = bf16[22,16,88]{2,0,1:T(8,128)(2,1)S(1)} async-done(((bf16[22,16,88]{2,0,1:T(8,128)(2,1)}), bf16[22,16,88]{2,0,1:T(8,128)(2,1)S(1)}, u32[]{:S(2)}, u32[]{:S(2)}) %all-to-all-start) | async-done | bytes 61984 | tf_op jit(solution)/shard_map/all_to_all | solution.py:56
  18.4 3.9 %all-to-all-start.3 = ((bf16[22,16,88]{2,0,1:T(8,128)(2,1)}), bf16[22,16,88]{2,0,1:T(8,128)(2,1)S(1)}, u32[]{:S(2)}, u32[]{:S(2)}) async-start(bf16[22,16,88]{2,0,1:T(8,128)(2,1)} %copy.92), calls=%async_computation.3 | async-start | bytes 196608 | tf_op jit(solution)/shard_map/all_to_all | solution.py:57
  23.2 5.0 %all-to-all-done.3 = bf16[22,16,88]{2,0,1:T(8,128)(2,1)S(1)} async-done(((bf16[22,16,88]{2,0,1:T(8,128)(2,1)}), bf16[22,16,88]{2,0,1:T(8,128)(2,1)S(1)}, u32[]{:S(2)}, u32[]{:S(2)}) %all-to-all-start.3) | async-done | bytes 61984 | tf_op jit(solution)/shard_map/all_to_all | solution.py:57
  28.2 3.9 %all-to-all-start.6 = ((bf16[22,16,88]{2,0,1:T(8,128)(2,1)}), bf16[22,16,88]{2,0,1:T(8,128)(2,1)S(1)}, u32[]{:S(2)}, u32[]{:S(2)}) async-start(bf16[22,16,88]{2,0,1:T(8,128)(2,1)} %copy.100), calls=%async_computation.6 | async-start | bytes 196608 | tf_op jit(solution)/shard_map/all_to_all | solution.py:58
  32.8 5.2 %all-to-all-done.6 = bf16[22,16,88]{2,0,1:T(8,128)(2,1)S(1)} async-done(((bf16[22,16,88]{2,0,1:T(8,128)(2,1)}), bf16[22,16,88]{2,0,1:T(8,128)(2,1)S(1)}, u32[]{:S(2)}, u32[]{:S(2)}) %all-to-all-start.6) | async-done | bytes 61984 | tf_op jit(solution)/shard_map/all_to_all | solution.py:58
  38.0 6.6 %all-to-all-start.1 = ((bf16[8,2,22,88]{3,1,2,0:T(2,128)(2,1)}), bf16[8,2,22,88]{3,1,2,0:T(2,128)(2,1)S(1)}, u32[]{:S(2)}, u32[]{:S(2)}) async-start(bf16[8,2,22,88]{3,1,2,0:T(2,128)(2,1)} %copy.86), calls=%async_computation.1 | async-start | bytes 180224 | tf_op jit(solution)/shard_map/all_to_all | solution.py:65
  45.4 6.8 %all-to-all-done.1 = bf16[8,2,22,88]{3,1,2,0:T(2,128)(2,1)S(1)} async-done(((bf16[8,2,22,88]{3,1,2,0:T(2,128)(2,1)}), bf16[8,2,22,88]{3,1,2,0:T(2,128)(2,1)S(1)}, u32[]{:S(2)}, u32[]{:S(2)}) %all-to-all-start.1) | async-done | bytes 61984 | tf_op jit(solution)/shard_map/all_to_all | solution.py:65
  52.1 3.4 %all-to-all-start.4 = ((bf16[8,2,22,88]{3,1,2,0:T(2,128)(2,1)}), bf16[8,2,22,88]{3,1,2,0:T(2,128)(2,1)S(1)}, u32[]{:S(2)}, u32[]{:S(2)}) async-start(bf16[8,2,22,88]{3,1,2,0:T(2,128)(2,1)} %copy.94), calls=%async_computation.4 | async-start | bytes 180224 | tf_op jit(solution)/shard_map/all_to_all | solution.py:65
  56.2 6.8 %all-to-all-done.4 = bf16[8,2,22,88]{3,1,2,0:T(2,128)(2,1)S(1)} async-done(((bf16[8,2,22,88]{3,1,2,0:T(2,128)(2,1)}), bf16[8,2,22,88]{3,1,2,0:T(2,128)(2,1)S(1)}, u32[]{:S(2)}, u32[]{:S(2)}) %all-to-all-start.4) | async-done | bytes 61984 | tf_op jit(solution)/shard_map/all_to_all | solution.py:65
  63.0 3.4 %all-to-all-start.7 = ((bf16[8,2,22,88]{3,1,2,0:T(2,128)(2,1)}), bf16[8,2,22,88]{3,1,2,0:T(2,128)(2,1)S(1)}, u32[]{:S(2)}, u32[]{:S(2)}) async-start(bf16[8,2,22,88]{3,1,2,0:T(2,128)(2,1)} %copy.102), calls=%async_computation.7 | async-start | bytes 180224 | tf_op jit(solution)/shard_map/all_to_all | solution.py:65
  67.1 6.7 %all-to-all-done.7 = bf16[8,2,22,88]{3,1,2,0:T(2,128)(2,1)S(1)} async-done(((bf16[8,2,22,88]{3,1,2,0:T(2,128)(2,1)}), bf16[8,2,22,88]{3,1,2,0:T(2,128)(2,1)S(1)}, u32[]{:S(2)}, u32[]{:S(2)}) %all-to-all-start.7) | async-done | bytes 61984 | tf_op jit(solution)/shard_map/all_to_all | solution.py:65
  73.8 5.9 %all-to-all-start.2 = ((bf16[4,4,1,22,88]{4,1,3,2,0:T(4,128)(2,1)}), bf16[4,4,1,22,88]{4,1,3,2,0:T(4,128)(2,1)S(1)}, u32[]{:S(2)}, u32[]{:S(2)}) async-start(bf16[4,4,1,22,88]{4,1,3,2,0:T(4,128)(2,1)} %copy.88), calls=%async_computation.2 | async-start | bytes 180224 | tf_op jit(solution)/shard_map/all_to_all | solution.py:73
  80.4 6.3 %all-to-all-done.2 = bf16[4,4,1,22,88]{4,1,3,2,0:T(4,128)(2,1)S(1)} async-done(((bf16[4,4,1,22,88]{4,1,3,2,0:T(4,128)(2,1)}), bf16[4,4,1,22,88]{4,1,3,2,0:T(4,128)(2,1)S(1)}, u32[]{:S(2)}, u32[]{:S(2)}) %all-to-all-start.2) | async-done | bytes 61984 | tf_op jit(solution)/shard_map/all_to_all | solution.py:73
  86.7 3.3 %all-to-all-start.5 = ((bf16[4,4,1,22,88]{4,1,3,2,0:T(4,128)(2,1)}), bf16[4,4,1,22,88]{4,1,3,2,0:T(4,128)(2,1)S(1)}, u32[]{:S(2)}, u32[]{:S(2)}) async-start(bf16[4,4,1,22,88]{4,1,3,2,0:T(4,128)(2,1)} %copy.96), calls=%async_computation.5 | async-start | bytes 180224 | tf_op jit(solution)/shard_map/all_to_all | solution.py:73
  91.7 3.8 %all_gather.27 = bf16[2,352,88]{1,2,0:T(8,128)(2,1)S(1)} all-gather(bf16[1,352,88]{1,2,0:T(8,128)(2,1)S(1)} %copy.90), channel_id=1, replica_groups=mesh['dp_0'=4,'dp_1'=2,'dp_2'=2,'pipe'=8,'tensor'=4] {'dp_1'}, dimensions={0}, use_global_device_ids=true | all-gather | bytes 185856 | tf_op jit(solution)/shard_map/all_gather | solution.py:25
  95.5 1.5 all-to-all-done.5
  97.0 5.1 %all-to-all-start.8 = ((bf16[4,4,1,22,88]{4,1,3,2,0:T(4,128)(2,1)}), bf16[4,4,1,22,88]{4,1,3,2,0:T(4,128)(2,1)S(1)}, u32[]{:S(2)}, u32[]{:S(2)}) async-start(bf16[4,4,1,22,88]{4,1,3,2,0:T(4,128)(2,1)} %copy.104), calls=%async_computation.8 | async-start | bytes 180224 | tf_op jit(solution)/shard_map/all_to_all | solution.py:73
  102.3 4.3 %all_gather.30 = bf16[2,352,88]{1,2,0:T(8,128)(2,1)S(1)} all-gather(bf16[1,352,88]{1,2,0:T(8,128)(2,1)S(1)} %copy.98), channel_id=1, replica_groups=mesh['dp_0'=4,'dp_1'=2,'dp_2'=2,'pipe'=8,'tensor'=4] {'dp_1'}, dimensions={0}, use_global_device_ids=true | all-gather | bytes 185856 | tf_op jit(solution)/shard_map/all_gather | solution.py:25
  106.5 10.5 %all_gather.31 = bf16[8,352,88]{1,2,0:T(8,128)(2,1)S(1)} all-gather(bf16[2,352,88]{1,2,0:T(8,128)(2,1)S(1)} %all_gather.30), channel_id=1, replica_groups=mesh['dp_0'=4,'dp_1'=2,'dp_2'=2,'pipe'=8,'tensor'=4] {'dp_0'}, dimensions={0}, use_global_device_ids=true | all-gather | bytes 619520 | tf_op jit(solution)/shard_map/all_gather | solution.py:25
  117.1 11.4 %all_gather.28 = bf16[8,352,88]{1,2,0:T(8,128)(2,1)S(1)} all-gather(bf16[2,352,88]{1,2,0:T(8,128)(2,1)S(1)} %all_gather.27), channel_id=1, replica_groups=mesh['dp_0'=4,'dp_1'=2,'dp_2'=2,'pipe'=8,'tensor'=4] {'dp_0'}, dimensions={0}, use_global_device_ids=true | all-gather | bytes 619520 | tf_op jit(solution)/shard_map/all_gather | solution.py:25
  128.4 15.4 %all_gather.29 = bf16[16,352,88]{1,2,0:T(8,128)(2,1)S(1)} all-gather(bf16[8,352,88]{1,2,0:T(8,128)(2,1)S(1)} %all_gather.28), channel_id=1, replica_groups=mesh['dp_0'=4,'dp_1'=2,'dp_2'=2,'pipe'=8,'tensor'=4] {'dp_2'}, dimensions={0}, use_global_device_ids=true | all-gather | bytes 1486848 | tf_op jit(solution)/shard_map/all_gather | solution.py:25
  143.9 1.9 %copy.108 = bf16[352,1408]{1,0:T(8,128)(2,1)} copy(bf16[352,1408]{0,1:T(8,128)(2,1)S(1)} %bitcast.77) | data formatting | bytes 1982464
  146.8 2.6 %all_gather.32 = bf16[16,352,88]{1,2,0:T(8,128)(2,1)S(1)} all-gather(bf16[8,352,88]{1,2,0:T(8,128)(2,1)S(1)} %all_gather.31), channel_id=1, replica_groups=mesh['dp_0'=4,'dp_1'=2,'dp_2'=2,'pipe'=8,'tensor'=4] {'dp_2'}, dimensions={0}, use_global_device_ids=true | all-gather | bytes 1486848 | tf_op jit(solution)/shard_map/all_gather | solution.py:25
  149.5 1.9 %copy.109 = bf16[352,1408]{1,0:T(8,128)(2,1)} copy(bf16[352,1408]{0,1:T(8,128)(2,1)S(1)} %bitcast.79) | data formatting | bytes 1982464
  152.6 3.8 %all_gather.33 = bf16[2,352,88]{1,2,0:T(8,128)(2,1)S(1)} all-gather(bf16[1,352,88]{1,2,0:T(8,128)(2,1)S(1)} %copy.106), channel_id=1, replica_groups=mesh['dp_0'=4,'dp_1'=2,'dp_2'=2,'pipe'=8,'tensor'=4] {'dp_1'}, dimensions={0}, use_global_device_ids=true | all-gather | bytes 185856 | tf_op jit(solution)/shard_map/all_gather | solution.py:25
  156.4 10.2 %all_gather.34 = bf16[8,352,88]{1,2,0:T(8,128)(2,1)S(1)} all-gather(bf16[2,352,88]{1,2,0:T(8,128)(2,1)S(1)} %all_gather.33), channel_id=1, replica_groups=mesh['dp_0'=4,'dp_1'=2,'dp_2'=2,'pipe'=8,'tensor'=4] {'dp_0'}, dimensions={0}, use_global_device_ids=true | all-gather | bytes 619520 | tf_op jit(solution)/shard_map/all_gather | solution.py:25
  166.6 6.7 %all_gather.35 = bf16[16,352,88]{1,2,0:T(8,128)(2,1)S(1)} all-gather(bf16[8,352,88]{1,2,0:T(8,128)(2,1)S(1)} %all_gather.34), channel_id=1, replica_groups=mesh['dp_0'=4,'dp_1'=2,'dp_2'=2,'pipe'=8,'tensor'=4] {'dp_2'}, dimensions={0}, use_global_device_ids=true | all-gather | bytes 1486848 | tf_op jit(solution)/shard_map/all_gather | solution.py:25
  173.4 1.0 convolution_reduce_fusion
  174.4 1.9 %copy.110 = bf16[352,1408]{1,0:T(8,128)(2,1)} copy(bf16[352,1408]{0,1:T(8,128)(2,1)S(1)} %bitcast.76) | data formatting | bytes 1982464
  (39 shorter events, 10.7 us)
Async XLA Ops:
  0.6 21.7 %copy-start = (bf16[22,1408]{1,0:T(8,128)(2,1)S(1)}, bf16[22,1408]{1,0:T(8,128)(2,1)}, u32[]{:S(2)}) copy-start(bf16[22,1408]{1,0:T(8,128)(2,1)} %param.7) | copy-start | bytes 185860
  2.4 16.0 %all-to-all-start = ((bf16[22,16,88]{2,0,1:T(8,128)(2,1)}), bf16[22,16,88]{2,0,1:T(8,128)(2,1)S(1)}, u32[]{:S(2)}, u32[]{:S(2)}) async-start(bf16[22,16,88]{2,0,1:T(8,128)(2,1)} %copy.84), calls=%async_computation | async-start | bytes 196608 | tf_op jit(solution)/shard_map/all_to_all | solution.py:56
  18.4 9.8 %all-to-all-start.3 = ((bf16[22,16,88]{2,0,1:T(8,128)(2,1)}), bf16[22,16,88]{2,0,1:T(8,128)(2,1)S(1)}, u32[]{:S(2)}, u32[]{:S(2)}) async-start(bf16[22,16,88]{2,0,1:T(8,128)(2,1)} %copy.92), calls=%async_computation.3 | async-start | bytes 196608 | tf_op jit(solution)/shard_map/all_to_all | solution.py:57
  28.2 9.8 %all-to-all-start.6 = ((bf16[22,16,88]{2,0,1:T(8,128)(2,1)}), bf16[22,16,88]{2,0,1:T(8,128)(2,1)S(1)}, u32[]{:S(2)}, u32[]{:S(2)}) async-start(bf16[22,16,88]{2,0,1:T(8,128)(2,1)} %copy.100), calls=%async_computation.6 | async-start | bytes 196608 | tf_op jit(solution)/shard_map/all_to_all | solution.py:58
  38.0 14.1 %all-to-all-start.1 = ((bf16[8,2,22,88]{3,1,2,0:T(2,128)(2,1)}), bf16[8,2,22,88]{3,1,2,0:T(2,128)(2,1)S(1)}, u32[]{:S(2)}, u32[]{:S(2)}) async-start(bf16[8,2,22,88]{3,1,2,0:T(2,128)(2,1)} %copy.86), calls=%async_computation.1 | async-start | bytes 180224 | tf_op jit(solution)/shard_map/all_to_all | solution.py:65
  52.1 10.9 %all-to-all-start.4 = ((bf16[8,2,22,88]{3,1,2,0:T(2,128)(2,1)}), bf16[8,2,22,88]{3,1,2,0:T(2,128)(2,1)S(1)}, u32[]{:S(2)}, u32[]{:S(2)}) async-start(bf16[8,2,22,88]{3,1,2,0:T(2,128)(2,1)} %copy.94), calls=%async_computation.4 | async-start | bytes 180224 | tf_op jit(solution)/shard_map/all_to_all | solution.py:65
  63.0 10.8 %all-to-all-start.7 = ((bf16[8,2,22,88]{3,1,2,0:T(2,128)(2,1)}), bf16[8,2,22,88]{3,1,2,0:T(2,128)(2,1)S(1)}, u32[]{:S(2)}, u32[]{:S(2)}) async-start(bf16[8,2,22,88]{3,1,2,0:T(2,128)(2,1)} %copy.102), calls=%async_computation.7 | async-start | bytes 180224 | tf_op jit(solution)/shard_map/all_to_all | solution.py:65
  73.8 12.9 %all-to-all-start.2 = ((bf16[4,4,1,22,88]{4,1,3,2,0:T(4,128)(2,1)}), bf16[4,4,1,22,88]{4,1,3,2,0:T(4,128)(2,1)S(1)}, u32[]{:S(2)}, u32[]{:S(2)}) async-start(bf16[4,4,1,22,88]{4,1,3,2,0:T(4,128)(2,1)} %copy.88), calls=%async_computation.2 | async-start | bytes 180224 | tf_op jit(solution)/shard_map/all_to_all | solution.py:73
  86.7 10.3 %all-to-all-start.5 = ((bf16[4,4,1,22,88]{4,1,3,2,0:T(4,128)(2,1)}), bf16[4,4,1,22,88]{4,1,3,2,0:T(4,128)(2,1)S(1)}, u32[]{:S(2)}, u32[]{:S(2)}) async-start(bf16[4,4,1,22,88]{4,1,3,2,0:T(4,128)(2,1)} %copy.96), calls=%async_computation.5 | async-start | bytes 180224 | tf_op jit(solution)/shard_map/all_to_all | solution.py:73
  97.0 55.4 %all-to-all-start.8 = ((bf16[4,4,1,22,88]{4,1,3,2,0:T(4,128)(2,1)}), bf16[4,4,1,22,88]{4,1,3,2,0:T(4,128)(2,1)S(1)}, u32[]{:S(2)}, u32[]{:S(2)}) async-start(bf16[4,4,1,22,88]{4,1,3,2,0:T(4,128)(2,1)} %copy.104), calls=%async_computation.8 | async-start | bytes 180224 | tf_op jit(solution)/shard_map/all_to_all | solution.py:73
  174.4 1.9 %copy-start.1 = (f32[1408]{0:T(1024)S(1)}, f32[1408]{0:T(1024)}, u32[]{:S(2)}) copy-start(f32[1408]{0:T(1024)} %param.9) | copy-start | bytes 16900
where the time goes:
time: 178 us; the launch traced here: 177 us
  blocking collectives  68.7 us (39%)
  starting transfers between devices  45.5 us (26%)
  waiting for transfers between devices  42.5 us (24%)
  local copies, waits for them, and re-layouts  15.8 us (9%)
  matrix products  2.99 us (2%)
    all_gather x9, blocking collectives, gather_in_order(): blocks = lax.all_gather(blocks, axes[k], axis=0, tiled=True)  68.7 us
    all_to_all x3, waiting for transfers between devices, shards(): lax.all_to_all(for_sending(grouped), 'pipe', split_axis=0, concat_axis=2,...  20.2 us
    all_to_all x3, starting transfers between devices, shards(): lax.all_to_all(for_sending(routed), 'tensor', split_axis=0, concat_axis=2...  14.3 us
    all_to_all x3, starting transfers between devices, shards(): lax.all_to_all(for_sending(grouped), 'pipe', split_axis=0, concat_axis=2,...  13.4 us
    all_to_all x1, starting transfers between devices, shards(): lax.all_to_all(sources[0], DP, split_axis=1, concat_axis=0, tiled=True)  10.1 us
    all_to_all x3, waiting for transfers between devices, shards(): lax.all_to_all(for_sending(routed), 'tensor', split_axis=0, concat_axis=2...  7.87 us
    unnamed x7, local copies, waits for them, and re-layouts  5.68 us
    all_to_all x1, waiting for transfers between devices, shards(): lax.all_to_all(sources[2], DP, split_axis=1, concat_axis=0, tiled=True)  5.18 us
  transfers between devices with their start and end apart: 9, of which 8 were waited for; matrix products, arithmetic and copies ran while one was open for 7% of the time, Pallas kernels for 0%

commit v1 on v0

--- a/solution.py
+++ b/solution.py
@@ -22,7 +22,9 @@
 def gather_in_order(array, axes, order):
     blocks = array[None]
     for k in order:
-        blocks = lax.all_gather(blocks, axes[k], axis=0, tiled=True)
+        blocks = jnp.concatenate(
+            lax.all_to_all(jnp.stack([blocks] * lax.axis_size(axes[k])), axes[k], 0, 0), axis=0
+        )
     block = [lax.axis_size(axes[k]) for k in reversed(order)]
     blocks = blocks.reshape(*block, *array.shape)
     turned = sorted(range(len(order)), key=lambda place: order[len(order) - 1 - place])

time: 178 us -> 200 us (1.12)
  waiting for transfers between devices: 42.5 us -> 70.3 us
  blocking collectives: 68.7 us -> 43.5 us
  starting transfers between devices: 45.5 us -> 58.2 us
  local copies, waits for them, and re-layouts: 15.8 us -> 19 us
  other arithmetic: 0.72 us -> 3.67 us
    all_gather x9 -> x0, blocking collectives: 68.7 us -> none  [gather_in_order(): blocks = lax.all_gather(blocks, axes[k], axis=0, tiled=True)]
    all_to_all x0 -> x5, blocking collectives: none -> 43.5 us  [gather_in_order(): lax.all_to_all(jnp.stack([blocks] * lax.axis_size(axes[k])), axes[k], 0, 0)]
    all_to_all x0 -> x4, waiting for transfers between devices: none -> 17 us  [gather_in_order(): lax.all_to_all(jnp.stack([blocks] * lax.axis_size(axes[k])), axes[k], 0, 0)]
    all_to_all x0 -> x4, starting transfers between devices: none -> 14.5 us  [gather_in_order(): lax.all_to_all(jnp.stack([blocks] * lax.axis_size(axes[k])), axes[k], 0, 0)]
    all_to_all x3, waiting for transfers between devices: 7.87 us -> 18.7 us  [shards(): lax.all_to_all(for_sending(routed), 'tensor', split_axis=0, concat_axis=2...]
    another operation x6 -> x9, local copies, waits for them, and re-layouts: 0.43 us -> 3.58 us  [gather_in_order(): jnp.stack([blocks] * lax.axis_size(axes[k]))]
    another operation x0 -> x6, other arithmetic: none -> 2.95 us  [gather_in_order(): jnp.stack([blocks] * lax.axis_size(axes[k]))]
    unnamed x7 -> x9, local copies, waits for them, and re-layouts: 5.68 us -> 5.68 us
  transfers between devices with their start and end apart: 9 -> 13, of which waited for: 8 -> 13; matrix products, arithmetic and copies ran while one was open for 7% -> 8% of each run, Pallas kernels for 0% -> 0%
where the time goes in v1:
time: 200 us; the launch traced here: 199 us
  waiting for transfers between devices  70.3 us (35%)
  starting transfers between devices  58.2 us (29%)
  blocking collectives  43.5 us (22%)
  local copies, waits for them, and re-layouts  19 us (10%)
  other arithmetic  3.67 us (2%)
  matrix products  2.99 us (1%)
    all_to_all x5, blocking collectives, gather_in_order(): lax.all_to_all(jnp.stack([blocks] * lax.axis_size(axes[k])), axes[k], 0, 0)  43.5 us
    all_to_all x3, waiting for transfers between devices, shards(): lax.all_to_all(for_sending(grouped), 'pipe', split_axis=0, concat_axis=2,...  20.2 us
    all_to_all x3, waiting for transfers between devices, shards(): lax.all_to_all(for_sending(routed), 'tensor', split_axis=0, concat_axis=2...  18.7 us
    all_to_all x4, waiting for transfers between devices, gather_in_order(): lax.all_to_all(jnp.stack([blocks] * lax.axis_size(axes[k])), axes[k], 0, 0)  17 us
    all_to_all x4, starting transfers between devices, gather_in_order(): lax.all_to_all(jnp.stack([blocks] * lax.axis_size(axes[k])), axes[k], 0, 0)  14.5 us
    all_to_all x3, starting transfers between devices, shards(): lax.all_to_all(for_sending(grouped), 'pipe', split_axis=0, concat_axis=2,...  13.4 us
    all_to_all x3, starting transfers between devices, shards(): lax.all_to_all(for_sending(routed), 'tensor', split_axis=0, concat_axis=2...  12.5 us
    all_to_all x1, starting transfers between devices, shards(): lax.all_to_all(sources[0], DP, split_axis=1, concat_axis=0, tiled=True)  10.1 us
  transfers between devices with their start and end apart: 13, of which 13 were waited for; matrix products, arithmetic and copies ran while one was open for 8% of the time, Pallas kernels for 0%

profile of v1, /device:TPU:1, one launch (start us, length us, event | category | flops | bytes accessed | tf_op | source)
XLA Modules:
  0.0 198.5 jit_solution(13129834600835587658)
XLA Ops:
  2.4 10.1 %all-to-all-start = ((bf16[22,16,88]{2,0,1:T(8,128)(2,1)}), bf16[22,16,88]{2,0,1:T(8,128)(2,1)S(1)}, u32[]{:S(2)}, u32[]{:S(2)}) async-start(bf16[22,16,88]{2,0,1:T(8,128)(2,1)} %copy.87), calls=%async_computation | async-start | bytes 196608 | tf_op jit(solution)/shard_map/all_to_all | solution.py:58
  14.3 4.2 %all-to-all-done = bf16[22,16,88]{2,0,1:T(8,128)(2,1)S(1)} async-done(((bf16[22,16,88]{2,0,1:T(8,128)(2,1)}), bf16[22,16,88]{2,0,1:T(8,128)(2,1)S(1)}, u32[]{:S(2)}, u32[]{:S(2)}) %all-to-all-start) | async-done | bytes 61984 | tf_op jit(solution)/shard_map/all_to_all | solution.py:58
  18.4 3.9 %all-to-all-start.6 = ((bf16[22,16,88]{2,0,1:T(8,128)(2,1)}), bf16[22,16,88]{2,0,1:T(8,128)(2,1)S(1)}, u32[]{:S(2)}, u32[]{:S(2)}) async-start(bf16[22,16,88]{2,0,1:T(8,128)(2,1)} %copy.95), calls=%async_computation.6 | async-start | bytes 196608 | tf_op jit(solution)/shard_map/all_to_all | solution.py:59
  23.2 5.0 %all-to-all-done.6 = bf16[22,16,88]{2,0,1:T(8,128)(2,1)S(1)} async-done(((bf16[22,16,88]{2,0,1:T(8,128)(2,1)}), bf16[22,16,88]{2,0,1:T(8,128)(2,1)S(1)}, u32[]{:S(2)}, u32[]{:S(2)}) %all-to-all-start.6) | async-done | bytes 61984 | tf_op jit(solution)/shard_map/all_to_all | solution.py:59
  28.2 3.9 %all-to-all-start.12 = ((bf16[22,16,88]{2,0,1:T(8,128)(2,1)}), bf16[22,16,88]{2,0,1:T(8,128)(2,1)S(1)}, u32[]{:S(2)}, u32[]{:S(2)}) async-start(bf16[22,16,88]{2,0,1:T(8,128)(2,1)} %copy.103), calls=%async_computation.12 | async-start | bytes 196608 | tf_op jit(solution)/shard_map/all_to_all | solution.py:60
  32.8 5.2 %all-to-all-done.12 = bf16[22,16,88]{2,0,1:T(8,128)(2,1)S(1)} async-done(((bf16[22,16,88]{2,0,1:T(8,128)(2,1)}), bf16[22,16,88]{2,0,1:T(8,128)(2,1)S(1)}, u32[]{:S(2)}, u32[]{:S(2)}) %all-to-all-start.12) | async-done | bytes 61984 | tf_op jit(solution)/shard_map/all_to_all | solution.py:60
  38.0 6.6 %all-to-all-start.1 = ((bf16[8,2,22,88]{3,1,2,0:T(2,128)(2,1)}), bf16[8,2,22,88]{3,1,2,0:T(2,128)(2,1)S(1)}, u32[]{:S(2)}, u32[]{:S(2)}) async-start(bf16[8,2,22,88]{3,1,2,0:T(2,128)(2,1)} %copy.89), calls=%async_computation.1 | async-start | bytes 180224 | tf_op jit(solution)/shard_map/all_to_all | solution.py:67
  45.4 6.8 %all-to-all-done.1 = bf16[8,2,22,88]{3,1,2,0:T(2,128)(2,1)S(1)} async-done(((bf16[8,2,22,88]{3,1,2,0:T(2,128)(2,1)}), bf16[8,2,22,88]{3,1,2,0:T(2,128)(2,1)S(1)}, u32[]{:S(2)}, u32[]{:S(2)}) %all-to-all-start.1) | async-done | bytes 61984 | tf_op jit(solution)/shard_map/all_to_all | solution.py:67
  52.1 3.4 %all-to-all-start.7 = ((bf16[8,2,22,88]{3,1,2,0:T(2,128)(2,1)}), bf16[8,2,22,88]{3,1,2,0:T(2,128)(2,1)S(1)}, u32[]{:S(2)}, u32[]{:S(2)}) async-start(bf16[8,2,22,88]{3,1,2,0:T(2,128)(2,1)} %copy.97), calls=%async_computation.7 | async-start | bytes 180224 | tf_op jit(solution)/shard_map/all_to_all | solution.py:67
  56.2 6.8 %all-to-all-done.7 = bf16[8,2,22,88]{3,1,2,0:T(2,128)(2,1)S(1)} async-done(((bf16[8,2,22,88]{3,1,2,0:T(2,128)(2,1)}), bf16[8,2,22,88]{3,1,2,0:T(2,128)(2,1)S(1)}, u32[]{:S(2)}, u32[]{:S(2)}) %all-to-all-start.7) | async-done | bytes 61984 | tf_op jit(solution)/shard_map/all_to_all | solution.py:67
  63.0 3.4 %all-to-all-start.13 = ((bf16[8,2,22,88]{3,1,2,0:T(2,128)(2,1)}), bf16[8,2,22,88]{3,1,2,0:T(2,128)(2,1)S(1)}, u32[]{:S(2)}, u32[]{:S(2)}) async-start(bf16[8,2,22,88]{3,1,2,0:T(2,128)(2,1)} %copy.105), calls=%async_computation.13 | async-start | bytes 180224 | tf_op jit(solution)/shard_map/all_to_all | solution.py:67
  67.1 6.7 %all-to-all-done.13 = bf16[8,2,22,88]{3,1,2,0:T(2,128)(2,1)S(1)} async-done(((bf16[8,2,22,88]{3,1,2,0:T(2,128)(2,1)}), bf16[8,2,22,88]{3,1,2,0:T(2,128)(2,1)S(1)}, u32[]{:S(2)}, u32[]{:S(2)}) %all-to-all-start.13) | async-done | bytes 61984 | tf_op jit(solution)/shard_map/all_to_all | solution.py:67
  73.8 5.9 %all-to-all-start.2 = ((bf16[4,4,1,22,88]{4,1,3,2,0:T(4,128)(2,1)}), bf16[4,4,1,22,88]{4,1,3,2,0:T(4,128)(2,1)S(1)}, u32[]{:S(2)}, u32[]{:S(2)}) async-start(bf16[4,4,1,22,88]{4,1,3,2,0:T(4,128)(2,1)} %copy.91), calls=%async_computation.2 | async-start | bytes 180224 | tf_op jit(solution)/shard_map/all_to_all | solution.py:75
  80.4 6.3 %all-to-all-done.2 = bf16[4,4,1,22,88]{4,1,3,2,0:T(4,128)(2,1)S(1)} async-done(((bf16[4,4,1,22,88]{4,1,3,2,0:T(4,128)(2,1)}), bf16[4,4,1,22,88]{4,1,3,2,0:T(4,128)(2,1)S(1)}, u32[]{:S(2)}, u32[]{:S(2)}) %all-to-all-start.2) | async-done | bytes 61984 | tf_op jit(solution)/shard_map/all_to_all | solution.py:75
  86.7 3.3 %all-to-all-start.8 = ((bf16[4,4,1,22,88]{4,1,3,2,0:T(4,128)(2,1)}), bf16[4,4,1,22,88]{4,1,3,2,0:T(4,128)(2,1)S(1)}, u32[]{:S(2)}, u32[]{:S(2)}) async-start(bf16[4,4,1,22,88]{4,1,3,2,0:T(4,128)(2,1)} %copy.99), calls=%async_computation.8 | async-start | bytes 180224 | tf_op jit(solution)/shard_map/all_to_all | solution.py:75
  90.8 6.2 %all-to-all-done.8 = bf16[4,4,1,22,88]{4,1,3,2,0:T(4,128)(2,1)S(1)} async-done(((bf16[4,4,1,22,88]{4,1,3,2,0:T(4,128)(2,1)}), bf16[4,4,1,22,88]{4,1,3,2,0:T(4,128)(2,1)S(1)}, u32[]{:S(2)}, u32[]{:S(2)}) %all-to-all-start.8) | async-done | bytes 61984 | tf_op jit(solution)/shard_map/all_to_all | solution.py:75
  97.0 3.3 %all-to-all-start.14 = ((bf16[4,4,1,22,88]{4,1,3,2,0:T(4,128)(2,1)}), bf16[4,4,1,22,88]{4,1,3,2,0:T(4,128)(2,1)S(1)}, u32[]{:S(2)}, u32[]{:S(2)}) async-start(bf16[4,4,1,22,88]{4,1,3,2,0:T(4,128)(2,1)} %copy.107), calls=%async_computation.14 | async-start | bytes 180224 | tf_op jit(solution)/shard_map/all_to_all | solution.py:75
  101.2 6.1 %all-to-all-done.14 = bf16[4,4,1,22,88]{4,1,3,2,0:T(4,128)(2,1)S(1)} async-done(((bf16[4,4,1,22,88]{4,1,3,2,0:T(4,128)(2,1)}), bf16[4,4,1,22,88]{4,1,3,2,0:T(4,128)(2,1)S(1)}, u32[]{:S(2)}, u32[]{:S(2)}) %all-to-all-start.14) | async-done | bytes 61984 | tf_op jit(solution)/shard_map/all_to_all | solution.py:75
  107.3 3.4 %all-to-all-start.3 = ((bf16[2,1,352,88]{2,3,1,0:T(8,128)(2,1)}), bf16[2,1,352,88]{2,3,1,0:T(8,128)(2,1)S(1)}, u32[]{:S(2)}, u32[]{:S(2)}) async-start(bf16[2,1,352,88]{2,3,1,0:T(8,128)(2,1)} %copy.93), calls=%async_computation.3 | async-start | bytes 270336 | tf_op jit(solution)/shard_map/all_to_all | solution.py:26
  111.0 3.4 %all-to-all-done.3 = bf16[2,1,352,88]{2,3,1,0:T(8,128)(2,1)S(1)} async-done(((bf16[2,1,352,88]{2,3,1,0:T(8,128)(2,1)}), bf16[2,1,352,88]{2,3,1,0:T(8,128)(2,1)S(1)}, u32[]{:S(2)}, u32[]{:S(2)}) %all-to-all-start.3) | async-done | bytes 123936 | tf_op jit(solution)/shard_map/all_to_all | solution.py:26
  114.4 5.7 %all_to_all.183 = bf16[2,1,352,88]{2,3,1,0:T(8,128)(2,1)S(1)} all-to-all(bf16[2,1,352,88]{2,3,1,0:T(8,128)(2,1)S(1)} %copy.101), channel_id=1, replica_groups=mesh['dp_0'=4,'dp_1'=2,'dp_2'=2,'pipe'=8,'tensor'=4] {'dp_1'}, dimensions={0} | all-to-all | bytes 247808 | tf_op jit(solution)/shard_map/all_to_all | solution.py:26
  120.1 9.4 %all_to_all.184 = bf16[4,2,352,88]{2,3,1,0:T(8,128)(2,1)S(1)} all-to-all(bf16[4,2,352,88]{2,3,1,0:T(8,128)(2,1)S(1)} %stack.40), channel_id=1, replica_groups=mesh['dp_0'=4,'dp_1'=2,'dp_2'=2,'pipe'=8,'tensor'=4] {'dp_0'}, dimensions={0} | all-to-all | bytes 991232 | tf_op jit(solution)/shard_map/all_to_all | solution.py:26
  130.4 3.5 %all-to-all-start.10 = ((bf16[4,2,352,88]{2,3,1,0:T(8,128)(2,1)}), bf16[4,2,352,88]{2,3,1,0:T(8,128)(2,1)S(1)}, u32[]{:S(2)}, u32[]{:S(2)}) async-start(bf16[4,2,352,88]{2,3,1,0:T(8,128)(2,1)} %stack.43), calls=%async_computation.10 | async-start | bytes 1081344 | tf_op jit(solution)/shard_map/all_to_all | solution.py:26
  135.0 8.8 %all-to-all-done.10 = bf16[4,2,352,88]{2,3,1,0:T(8,128)(2,1)S(1)} async-done(((bf16[4,2,352,88]{2,3,1,0:T(8,128)(2,1)}), bf16[4,2,352,88]{2,3,1,0:T(8,128)(2,1)S(1)}, u32[]{:S(2)}, u32[]{:S(2)}) %all-to-all-start.10) | async-done | bytes 495648 | tf_op jit(solution)/shard_map/all_to_all | solution.py:26
  143.8 3.4 %all-to-all-start.15 = ((bf16[2,1,352,88]{2,3,1,0:T(8,128)(2,1)}), bf16[2,1,352,88]{2,3,1,0:T(8,128)(2,1)S(1)}, u32[]{:S(2)}, u32[]{:S(2)}) async-start(bf16[2,1,352,88]{2,3,1,0:T(8,128)(2,1)} %copy.109), calls=%async_computation.15 | async-start | bytes 270336 | tf_op jit(solution)/shard_map/all_to_all | solution.py:26
  148.4 2.1 %all-to-all-done.15 = bf16[2,1,352,88]{2,3,1,0:T(8,128)(2,1)S(1)} async-done(((bf16[2,1,352,88]{2,3,1,0:T(8,128)(2,1)}), bf16[2,1,352,88]{2,3,1,0:T(8,128)(2,1)S(1)}, u32[]{:S(2)}, u32[]{:S(2)}) %all-to-all-start.15) | async-done | bytes 123936 | tf_op jit(solution)/shard_map/all_to_all | solution.py:26
  150.6 18.3 %all_to_all.185 = bf16[2,8,352,88]{2,3,1,0:T(8,128)(2,1)S(1)} all-to-all(bf16[2,8,352,88]{2,3,1,0:T(8,128)(2,1)S(1)} %pad_maximum_fusion), channel_id=1, replica_groups=mesh['dp_0'=4,'dp_1'=2,'dp_2'=2,'pipe'=8,'tensor'=4] {'dp_2'}, dimensions={0} | all-to-all | bytes 1982464 | tf_op jit(solution)/shard_map/all_to_all | solution.py:26
  168.9 4.6 %all_to_all.186 = bf16[2,8,352,88]{2,3,1,0:T(8,128)(2,1)S(1)} all-to-all(bf16[2,8,352,88]{2,3,1,0:T(8,128)(2,1)S(1)} %copy-done), channel_id=1, replica_groups=mesh['dp_0'=4,'dp_1'=2,'dp_2'=2,'pipe'=8,'tensor'=4] {'dp_2'}, dimensions={0} | all-to-all | bytes 1982464 | tf_op jit(solution)/shard_map/all_to_all | solution.py:26
  174.3 4.2 %all-to-all-start.16 = ((bf16[4,2,352,88]{2,3,1,0:T(8,128)(2,1)}), bf16[4,2,352,88]{2,3,1,0:T(8,128)(2,1)}, u32[]{:S(2)}, u32[]{:S(2)}) async-start(bf16[4,2,352,88]{2,3,1,0:T(8,128)(2,1)} %stack.46), calls=%async_computation.16 | async-start | bytes 1081344 | tf_op jit(solution)/shard_map/all_to_all | solution.py:26
  179.4 1.9 copy.111
  185.3 2.6 %all-to-all-done.16 = bf16[4,2,352,88]{2,3,1,0:T(8,128)(2,1)} async-done(((bf16[4,2,352,88]{2,3,1,0:T(8,128)(2,1)}), bf16[4,2,352,88]{2,3,1,0:T(8,128)(2,1)}, u32[]{:S(2)}, u32[]{:S(2)}) %all-to-all-start.16) | async-done | bytes 495648 | tf_op jit(solution)/shard_map/all_to_all | solution.py:26
  189.3 5.4 %all_to_all.187 = bf16[2,8,352,88]{2,3,1,0:T(8,128)(2,1)S(1)} all-to-all(bf16[2,8,352,88]{2,3,1,0:T(8,128)(2,1)S(1)} %pad_maximum_fusion.2), channel_id=1, replica_groups=mesh['dp_0'=4,'dp_1'=2,'dp_2'=2,'pipe'=8,'tensor'=4] {'dp_2'}, dimensions={0} | all-to-all | bytes 1982464 | tf_op jit(solution)/shard_map/all_to_all | solution.py:26
  (54 shorter events, 23.8 us)
Async XLA Ops:
  0.6 21.7 %copy-start.1 = (bf16[22,1408]{1,0:T(8,128)(2,1)S(1)}, bf16[22,1408]{1,0:T(8,128)(2,1)}, u32[]{:S(2)}) copy-start(bf16[22,1408]{1,0:T(8,128)(2,1)} %param.7) | copy-start | bytes 185860
  2.4 16.0 %all-to-all-start = ((bf16[22,16,88]{2,0,1:T(8,128)(2,1)}), bf16[22,16,88]{2,0,1:T(8,128)(2,1)S(1)}, u32[]{:S(2)}, u32[]{:S(2)}) async-start(bf16[22,16,88]{2,0,1:T(8,128)(2,1)} %copy.87), calls=%async_computation | async-start | bytes 196608 | tf_op jit(solution)/shard_map/all_to_all | solution.py:58
  18.4 9.8 %all-to-all-start.6 = ((bf16[22,16,88]{2,0,1:T(8,128)(2,1)}), bf16[22,16,88]{2,0,1:T(8,128)(2,1)S(1)}, u32[]{:S(2)}, u32[]{:S(2)}) async-start(bf16[22,16,88]{2,0,1:T(8,128)(2,1)} %copy.95), calls=%async_computation.6 | async-start | bytes 196608 | tf_op jit(solution)/shard_map/all_to_all | solution.py:59
  28.2 9.8 %all-to-all-start.12 = ((bf16[22,16,88]{2,0,1:T(8,128)(2,1)}), bf16[22,16,88]{2,0,1:T(8,128)(2,1)S(1)}, u32[]{:S(2)}, u32[]{:S(2)}) async-start(bf16[22,16,88]{2,0,1:T(8,128)(2,1)} %copy.103), calls=%async_computation.12 | async-start | bytes 196608 | tf_op jit(solution)/shard_map/all_to_all | solution.py:60
  38.0 14.1 %all-to-all-start.1 = ((bf16[8,2,22,88]{3,1,2,0:T(2,128)(2,1)}), bf16[8,2,22,88]{3,1,2,0:T(2,128)(2,1)S(1)}, u32[]{:S(2)}, u32[]{:S(2)}) async-start(bf16[8,2,22,88]{3,1,2,0:T(2,128)(2,1)} %copy.89), calls=%async_computation.1 | async-start | bytes 180224 | tf_op jit(solution)/shard_map/all_to_all | solution.py:67
  52.1 10.9 %all-to-all-start.7 = ((bf16[8,2,22,88]{3,1,2,0:T(2,128)(2,1)}), bf16[8,2,22,88]{3,1,2,0:T(2,128)(2,1)S(1)}, u32[]{:S(2)}, u32[]{:S(2)}) async-start(bf16[8,2,22,88]{3,1,2,0:T(2,128)(2,1)} %copy.97), calls=%async_computation.7 | async-start | bytes 180224 | tf_op jit(solution)/shard_map/all_to_all | solution.py:67
  63.0 10.8 %all-to-all-start.13 = ((bf16[8,2,22,88]{3,1,2,0:T(2,128)(2,1)}), bf16[8,2,22,88]{3,1,2,0:T(2,128)(2,1)S(1)}, u32[]{:S(2)}, u32[]{:S(2)}) async-start(bf16[8,2,22,88]{3,1,2,0:T(2,128)(2,1)} %copy.105), calls=%async_computation.13 | async-start | bytes 180224 | tf_op jit(solution)/shard_map/all_to_all | solution.py:67
  73.8 12.9 %all-to-all-start.2 = ((bf16[4,4,1,22,88]{4,1,3,2,0:T(4,128)(2,1)}), bf16[4,4,1,22,88]{4,1,3,2,0:T(4,128)(2,1)S(1)}, u32[]{:S(2)}, u32[]{:S(2)}) async-start(bf16[4,4,1,22,88]{4,1,3,2,0:T(4,128)(2,1)} %copy.91), calls=%async_computation.2 | async-start | bytes 180224 | tf_op jit(solution)/shard_map/all_to_all | solution.py:75
  86.7 10.3 %all-to-all-start.8 = ((bf16[4,4,1,22,88]{4,1,3,2,0:T(4,128)(2,1)}), bf16[4,4,1,22,88]{4,1,3,2,0:T(4,128)(2,1)S(1)}, u32[]{:S(2)}, u32[]{:S(2)}) async-start(bf16[4,4,1,22,88]{4,1,3,2,0:T(4,128)(2,1)} %copy.99), calls=%async_computation.8 | async-start | bytes 180224 | tf_op jit(solution)/shard_map/all_to_all | solution.py:75
  97.0 10.3 %all-to-all-start.14 = ((bf16[4,4,1,22,88]{4,1,3,2,0:T(4,128)(2,1)}), bf16[4,4,1,22,88]{4,1,3,2,0:T(4,128)(2,1)S(1)}, u32[]{:S(2)}, u32[]{:S(2)}) async-start(bf16[4,4,1,22,88]{4,1,3,2,0:T(4,128)(2,1)} %copy.107), calls=%async_computation.14 | async-start | bytes 180224 | tf_op jit(solution)/shard_map/all_to_all | solution.py:75
  107.3 7.1 %all-to-all-start.3 = ((bf16[2,1,352,88]{2,3,1,0:T(8,128)(2,1)}), bf16[2,1,352,88]{2,3,1,0:T(8,128)(2,1)S(1)}, u32[]{:S(2)}, u32[]{:S(2)}) async-start(bf16[2,1,352,88]{2,3,1,0:T(8,128)(2,1)} %copy.93), calls=%async_computation.3 | async-start | bytes 270336 | tf_op jit(solution)/shard_map/all_to_all | solution.py:26
  130.4 13.4 %all-to-all-start.10 = ((bf16[4,2,352,88]{2,3,1,0:T(8,128)(2,1)}), bf16[4,2,352,88]{2,3,1,0:T(8,128)(2,1)S(1)}, u32[]{:S(2)}, u32[]{:S(2)}) async-start(bf16[4,2,352,88]{2,3,1,0:T(8,128)(2,1)} %stack.43), calls=%async_computation.10 | async-start | bytes 1081344 | tf_op jit(solution)/shard_map/all_to_all | solution.py:26
  143.8 6.8 %all-to-all-start.15 = ((bf16[2,1,352,88]{2,3,1,0:T(8,128)(2,1)}), bf16[2,1,352,88]{2,3,1,0:T(8,128)(2,1)S(1)}, u32[]{:S(2)}, u32[]{:S(2)}) async-start(bf16[2,1,352,88]{2,3,1,0:T(8,128)(2,1)} %copy.109), calls=%async_computation.15 | async-start | bytes 270336 | tf_op jit(solution)/shard_map/all_to_all | solution.py:26
  150.6 18.3 %copy-start = (bf16[2,8,352,88]{2,3,1,0:T(8,128)(2,1)S(1)}, bf16[2,8,352,88]{2,3,1,0:T(8,128)(2,1)}, u32[]{:S(2)}) copy-start(bf16[2,8,352,88]{2,3,1,0:T(8,128)(2,1)} %pad_maximum_fusion.1) | copy-start | bytes 2973700
  174.3 13.6 %all-to-all-start.16 = ((bf16[4,2,352,88]{2,3,1,0:T(8,128)(2,1)}), bf16[4,2,352,88]{2,3,1,0:T(8,128)(2,1)}, u32[]{:S(2)}, u32[]{:S(2)}) async-start(bf16[4,2,352,88]{2,3,1,0:T(8,128)(2,1)} %stack.46), calls=%async_computation.16 | async-start | bytes 1081344 | tf_op jit(solution)/shard_map/all_to_all | solution.py:26
  195.9 1.9 copy-start.2
